TPU v7x, 128 devices: a whole 4x4x4 slice. The times are simulated.
128 devices in a mesh: row: 16 (over x, z), col: 8 (over y, core).
Axes of the slice: x: 4, y: 4, z: 4, core: 2. Of those that a mesh axis runs over, the one named last changes fastest.
Arguments:
- old_params: float32 [2, 256, 32768], P(None, ('row', 'col')), may hold values from -0.12 to 0.12
- old_first: float32 [2, 256, 32768], P(None, ('row', 'col')), may hold values from -1.8 to 1.8
- old_second: float32 [2, 256, 32768], P(None, ('row', 'col')), may hold values from 0.001 to 1
- gradients: float32 [2, 128, 65536], P(None, ('row', 'col')), may hold values from -250 to 250
- old_table: int32 [2, 256], replicated, may hold values from 0 to 255, as said below
- new_table: int32 [2, 128], replicated, may hold values from 0 to 127, as said below
Outputs:
- new_params: float32 [2, 128, 65536], P(None, ('row', 'col'))
- new_first: float32 [2, 128, 65536], P(None, ('row', 'col'))
- new_second: float32 [2, 128, 65536], P(None, ('row', 'col'))
Inputs may be any that keep to these rules, and one draw needn't show every extreme that they name: old_table[t, p] = p XOR k for one k per tensor. new_table[t, q] = q XOR k for one k per tensor.
All inputs are finite; a program needn't handle non-finite values.
Results may differ from a plain program's by a relative error of at most 0.00002.
Values sent between devices are 32-bit elements; how exact they have to be, the bound alone decides.
A program may use at most 64 MiB of HBM per device.

v0:
```python
import math
import jax
import jax.numpy as jnp
from jax import lax
from jax.sharding import Mesh
from jax.sharding import PartitionSpec as P

STEP = 100
ROW_COL = ("row_0", "row_1", "col_0", "col_1")
beta_one = 0.9
beta_two = 0.95
epsilon = 1e-08
learn_rate = 0.001
decay_rate = 0.1


def one_axis_at_a_time(array, axes):
    for axis in axes:
        array = lax.psum(array, axis)
    return array


def from_partner(array, axis, apart):
    return lax.ppermute(array, axis, [(i, i ^ 1 << apart) for i in range(lax.axis_size(axis))])


def adam_update(params, first_moment, second_moment, gradients, clip_factor):
    scaled = clip_factor * gradients
    first_new = beta_one * first_moment + (1.0 - beta_one) * scaled
    second_new = beta_two * second_moment + (1.0 - beta_two) * scaled * scaled
    bias_first = 1.0 - beta_one**STEP
    bias_second = 1.0 - beta_two**STEP
    update = first_new / bias_first / (jnp.sqrt(second_new / bias_second) + epsilon)
    params_new = params - learn_rate * (update + decay_rate * params)
    return (params_new, first_new, second_new)


def global_clip(gradients):
    total_squares = one_axis_at_a_time(jnp.sum(gradients * gradients), ROW_COL)
    count = gradients.size * lax.axis_size(ROW_COL)
    limit = jnp.float32(0.5 * math.sqrt(count))
    return limit / jnp.maximum(jnp.sqrt(total_squares), limit)


def move_state(content, route_key):
    bit_total = lax.axis_size(ROW_COL).bit_length() - 1
    for bit_number in range(bit_total):
        flagged = jnp.bitwise_and(jnp.right_shift(route_key, bit_number), 1) == 1
        needed = jnp.any(flagged)

        def do_swap(state, flagged=flagged, bit_number=bit_number):
            received = from_partner(state, ROW_COL, bit_number)
            return jnp.where(flagged[None, :, None, None], received, state)

        def keep_state(state):
            return state

        content = lax.cond(needed, do_swap, keep_state, content)
    return content


def shards(old_params, old_first, old_second, gradients, old_table, new_table):
    old_key = old_table[:, 0]
    route_key = jnp.bitwise_xor(jnp.right_shift(old_key, 1), new_table[:, 0])
    content = jnp.stack([old_params, old_first, old_second])
    swapped = content[:, :, ::-1, :]
    low_set = jnp.bitwise_and(old_key, 1) == 1
    content = jnp.where(low_set[None, :, None, None], swapped, content)
    content = move_state(content, route_key)
    clip_factor = global_clip(gradients)
    shaped = content.reshape(3, content.shape[1], 1, 2 * content.shape[3])
    return adam_update(shaped[0], shaped[1], shaped[2], gradients, clip_factor)


def solution(mesh):
    finer = Mesh(mesh.devices.reshape(4, 4, 4, 2), ("row_0", "row_1", "col_0", "col_1"))
    in_specs = (
        P(None, ROW_COL, None),
        P(None, ROW_COL, None),
        P(None, ROW_COL, None),
        P(None, ROW_COL, None),
        P(),
        P(),
    )
    out_specs = (P(None, ROW_COL, None), P(None, ROW_COL, None), P(None, ROW_COL, None))
    return jax.shard_map(
        shards, mesh=finer, in_specs=in_specs, out_specs=out_specs, check_vma=False
    )
```

profile of v0, /device:TPU:1, one launch (start us, length us, event | category | flops | bytes accessed | tf_op | source)
XLA Modules:
  0.0 250.2 jit_solution(17393433382442638120)
XLA Ops:
  0.6 2.0 pad_maximum_fusion
  2.7 9.7 %rev.3 = f32[3,2,2,32768]{3,2,1,0:T(2,128)S(1)} reverse(f32[3,2,2,32768]{3,2,1,0:T(2,128)S(1)} %pad_maximum_fusion), dimensions={2} | reverse | bytes 3145728 | tf_op jit(solution)/shard_map/rev | solution.py:66
  13.1 2.2 broadcast_select_fusion.7
  17.4 36.9 %conditional.8 = (f32[3,2,2,32768]{3,2,1,0:T(2,128)S(1)}) conditional(s32[]{:T(128)} %convert_element_type.26, f32[3,2,2,32768]{3,2,1,0:T(2,128)S(1)} %get-tuple-element.112, (pred[2,1]{1,0:T(4,128)(4,1)S(1)}, f32[3,2,2,32768]{3,2,1,0:T(2,128)S(1)}) %tuple.51), branch_computations={%region_9.10_spmd, %region_10.11_spmd} | conditional | flops 393216 | bytes 11010103 | solution.py:58
  17.4 2.2 collective-permute-start.1
  19.7 33.6 %collective-permute-done.1 = f32[3,2,2,32768]{3,2,1,0:T(2,128)S(1)} collective-permute-done((f32[3,2,2,32768]{3,2,1,0:T(2,128)S(1)}, f32[3,2,2,32768]{3,2,1,0:T(2,128)S(1)}, u32[]{:S(2)}, u32[]{:S(2)}) %collective-permute-start.1) | collective-permute-done | bytes 1572896 | tf_op jit(solution)/shard_map/cond/branch_1_fun/ppermute | solution.py:24
  55.0 37.3 %conditional.9 = (f32[3,2,2,32768]{3,2,1,0:T(2,128)S(1)}) conditional(s32[]{:T(128)} %convert_element_type.25, f32[3,2,2,32768]{3,2,1,0:T(2,128)S(1)} %get-tuple-element.113, (pred[2,1]{1,0:T(4,128)(4,1)S(1)}, f32[3,2,2,32768]{3,2,1,0:T(2,128)S(1)}) %tuple.52), branch_computations={%region_11.12_spmd, %region_12.13_spmd} | conditional | flops 393216 | bytes 11010103 | solution.py:58
  55.0 3.2 %collective-permute-start.2 = (f32[3,2,2,32768]{3,2,1,0:T(2,128)S(1)}, f32[3,2,2,32768]{3,2,1,0:T(2,128)S(1)}, u32[]{:S(2)}, u32[]{:S(2)}) collective-permute-start(f32[3,2,2,32768]{3,2,1,0:T(2,128)S(1)} %get-tuple-element.61), channel_id=1, source_target_pairs={{0,4},{1,5},{2,6},{3,7},{4,0},{5,1},{6,2},{7,3},{8,12},{9,13},{10,... | collective-permute-start | bytes 4718600 | tf_op jit(solution)/shard_map/cond/branch_1_fun/ppermute | solution.py:24
  58.4 33.0 %collective-permute-done.2 = f32[3,2,2,32768]{3,2,1,0:T(2,128)S(1)} collective-permute-done((f32[3,2,2,32768]{3,2,1,0:T(2,128)S(1)}, f32[3,2,2,32768]{3,2,1,0:T(2,128)S(1)}, u32[]{:S(2)}, u32[]{:S(2)}) %collective-permute-start.2) | collective-permute-done | bytes 1572896 | tf_op jit(solution)/shard_map/cond/branch_1_fun/ppermute | solution.py:24
  92.9 35.0 %conditional.10 = (f32[3,2,2,32768]{3,2,1,0:T(2,128)S(1)}) conditional(s32[]{:T(128)} %convert_element_type.24, f32[3,2,2,32768]{3,2,1,0:T(2,128)S(1)} %get-tuple-element.114, (pred[2,1]{1,0:T(4,128)(4,1)S(1)}, f32[3,2,2,32768]{3,2,1,0:T(2,128)S(1)}) %tuple.53), branch_computations={%region_13.14_spmd, %region_14.15_spmd} | conditional | flops 393216 | bytes 11010103 | solution.py:58
  93.0 1.7 collective-permute-start.3
  94.7 32.2 %collective-permute-done.3 = f32[3,2,2,32768]{3,2,1,0:T(2,128)S(1)} collective-permute-done((f32[3,2,2,32768]{3,2,1,0:T(2,128)S(1)}, f32[3,2,2,32768]{3,2,1,0:T(2,128)S(1)}, u32[]{:S(2)}, u32[]{:S(2)}) %collective-permute-start.3) | collective-permute-done | bytes 1572896 | tf_op jit(solution)/shard_map/cond/branch_1_fun/ppermute | solution.py:24
  128.6 35.8 %conditional.11 = (f32[3,2,2,32768]{3,2,1,0:T(2,128)S(1)}) conditional(s32[]{:T(128)} %convert_element_type.23, f32[3,2,2,32768]{3,2,1,0:T(2,128)S(1)} %get-tuple-element.115, (pred[2,1]{1,0:T(4,128)(4,1)S(1)}, f32[3,2,2,32768]{3,2,1,0:T(2,128)S(1)}) %tuple.54), branch_computations={%region_15.16_spmd, %region_16.17_spmd} | conditional | flops 393216 | bytes 11010103 | solution.py:58
  128.6 3.3 %collective-permute-start.4 = (f32[3,2,2,32768]{3,2,1,0:T(2,128)S(1)}, f32[3,2,2,32768]{3,2,1,0:T(2,128)S(1)}, u32[]{:S(2)}, u32[]{:S(2)}) collective-permute-start(f32[3,2,2,32768]{3,2,1,0:T(2,128)S(1)} %get-tuple-element.65), channel_id=1, source_target_pairs={{0,16},{1,17},{2,18},{3,19},{4,20},{5,21},{6,22},{7,23},{8,24},{9,... | collective-permute-start | bytes 4718600 | tf_op jit(solution)/shard_map/cond/branch_1_fun/ppermute | solution.py:24
  132.0 31.4 %collective-permute-done.4 = f32[3,2,2,32768]{3,2,1,0:T(2,128)S(1)} collective-permute-done((f32[3,2,2,32768]{3,2,1,0:T(2,128)S(1)}, f32[3,2,2,32768]{3,2,1,0:T(2,128)S(1)}, u32[]{:S(2)}, u32[]{:S(2)}) %collective-permute-start.4) | collective-permute-done | bytes 1572896 | tf_op jit(solution)/shard_map/cond/branch_1_fun/ppermute | solution.py:24
  165.0 33.2 %conditional.12 = (f32[3,2,2,32768]{3,2,1,0:T(2,128)S(1)}) conditional(s32[]{:T(128)} %convert_element_type.22, f32[3,2,2,32768]{3,2,1,0:T(2,128)S(1)} %get-tuple-element.116, (pred[2,1]{1,0:T(4,128)(4,1)S(1)}, f32[3,2,2,32768]{3,2,1,0:T(2,128)S(1)}) %tuple.55), branch_computations={%region_17.18_spmd, %region_18.19_spmd} | conditional | flops 393216 | bytes 11010103 | solution.py:58
  165.0 1.3 collective-permute-start.5
  166.4 30.8 %collective-permute-done.5 = f32[3,2,2,32768]{3,2,1,0:T(2,128)S(1)} collective-permute-done((f32[3,2,2,32768]{3,2,1,0:T(2,128)S(1)}, f32[3,2,2,32768]{3,2,1,0:T(2,128)S(1)}, u32[]{:S(2)}, u32[]{:S(2)}) %collective-permute-start.5) | collective-permute-done | bytes 1572896 | tf_op jit(solution)/shard_map/cond/branch_1_fun/ppermute | solution.py:24
  202.2 1.7 multiply_reduce_fusion
  203.9 9.1 %psum.28 = f32[]{:T(128)} all-reduce(f32[]{:T(128)} %multiply_reduce_fusion), channel_id=1, replica_groups=mesh['row_0'=4,'row_1'=4,'col_0'=4,'col_1'=2] {'row_0'}, use_global_device_ids=true, to_apply=%region_22.23 | all-reduce | flops 1 | bytes 8 | tf_op jit(solution)/shard_map/psum | solution.py:19
  213.0 9.2 %psum.29 = f32[]{:T(128)} all-reduce(f32[]{:T(128)} %psum.28), channel_id=1, replica_groups=mesh['row_0'=4,'row_1'=4,'col_0'=4,'col_1'=2] {'row_1'}, use_global_device_ids=true, to_apply=%region_23.24 | all-reduce | flops 1 | bytes 8 | tf_op jit(solution)/shard_map/psum | solution.py:19
  222.1 9.3 %psum.30 = f32[]{:T(128)} all-reduce(f32[]{:T(128)} %psum.29), channel_id=1, replica_groups=mesh['row_0'=4,'row_1'=4,'col_0'=4,'col_1'=2] {'col_0'}, use_global_device_ids=true, to_apply=%region_24.25 | all-reduce | flops 1 | bytes 8 | tf_op jit(solution)/shard_map/psum | solution.py:19
  231.4 13.7 %psum.31 = f32[]{:T(128)} all-reduce(f32[]{:T(128)} %psum.30), channel_id=1, replica_groups=mesh['row_0'=4,'row_1'=4,'col_0'=4,'col_1'=2] {'col_1'}, use_global_device_ids=true, to_apply=%region_25.26 | all-reduce | flops 1 | bytes 8 | tf_op jit(solution)/shard_map/psum | solution.py:19
  245.9 4.3 %multiply_subtract_fusion = (f32[2,1,65536]{2,1,0:T(1,128)}, f32[2,1,65536]{2,1,0:T(1,128)}, f32[2,1,65536]{2,1,0:T(1,128)}) fusion(f32[2,1,65536]{2,1,0:T(1,128)S(1)} %squeeze.2, f32[2,1,65536]{2,1,0:T(1,128)S(1)} %mul.74, f32[2,1,65536]{2,1,0:T(1,128)S(1)} %copy-done, f32[]{:T(128)S(6)} %div.18, f32[2,1,65536]{2,1,0:T(1,128)S(1)} %mul.81), kind=kLoop, calls=%fused_computation.13 | loop fusion | flops 1835008 | bytes 3670020 | tf_op jit(solution)/shard_map/sub | solution.py:34
  (24 shorter events, 10.2 us)
Async XLA Ops:
  2.7 9.8 %copy-start.1 = (s32[2,128]{1,0:T(2,128)S(1)}, s32[2,128]{1,0:T(2,128)}, u32[]{:S(2)}) copy-start(s32[2,128]{1,0:T(2,128)} %param.25) | copy-start | bytes 3076
  2.7 9.8 %copy-start.2 = (s32[2,256]{1,0:T(2,128)S(1)}, s32[2,256]{1,0:T(2,128)}, u32[]{:S(2)}) copy-start(s32[2,256]{1,0:T(2,128)} %param.24) | copy-start | bytes 6148
  17.4 36.0 %collective-permute-start.1 = (f32[3,2,2,32768]{3,2,1,0:T(2,128)S(1)}, f32[3,2,2,32768]{3,2,1,0:T(2,128)S(1)}, u32[]{:S(2)}, u32[]{:S(2)}) collective-permute-start(f32[3,2,2,32768]{3,2,1,0:T(2,128)S(1)} %get-tuple-element.59), channel_id=1, source_target_pairs={{0,2},{1,3},{2,0},{3,1},{4,6},{5,7},{6,4},{7,5},{8,10},{9,11},{10,... | collective-permute-start | bytes 4718600 | tf_op jit(solution)/shard_map/cond/branch_1_fun/ppermute | solution.py:24
  55.0 36.3 %collective-permute-start.2 = (f32[3,2,2,32768]{3,2,1,0:T(2,128)S(1)}, f32[3,2,2,32768]{3,2,1,0:T(2,128)S(1)}, u32[]{:S(2)}, u32[]{:S(2)}) collective-permute-start(f32[3,2,2,32768]{3,2,1,0:T(2,128)S(1)} %get-tuple-element.61), channel_id=1, source_target_pairs={{0,4},{1,5},{2,6},{3,7},{4,0},{5,1},{6,2},{7,3},{8,12},{9,13},{10,... | collective-permute-start | bytes 4718600 | tf_op jit(solution)/shard_map/cond/branch_1_fun/ppermute | solution.py:24
  93.0 34.0 %collective-permute-start.3 = (f32[3,2,2,32768]{3,2,1,0:T(2,128)S(1)}, f32[3,2,2,32768]{3,2,1,0:T(2,128)S(1)}, u32[]{:S(2)}, u32[]{:S(2)}) collective-permute-start(f32[3,2,2,32768]{3,2,1,0:T(2,128)S(1)} %get-tuple-element.63), channel_id=1, source_target_pairs={{0,8},{1,9},{2,10},{3,11},{4,12},{5,13},{6,14},{7,15},{8,0},{9,1},... | collective-permute-start | bytes 4718600 | tf_op jit(solution)/shard_map/cond/branch_1_fun/ppermute | solution.py:24
  128.6 34.8 %collective-permute-start.4 = (f32[3,2,2,32768]{3,2,1,0:T(2,128)S(1)}, f32[3,2,2,32768]{3,2,1,0:T(2,128)S(1)}, u32[]{:S(2)}, u32[]{:S(2)}) collective-permute-start(f32[3,2,2,32768]{3,2,1,0:T(2,128)S(1)} %get-tuple-element.65), channel_id=1, source_target_pairs={{0,16},{1,17},{2,18},{3,19},{4,20},{5,21},{6,22},{7,23},{8,24},{9,... | collective-permute-start | bytes 4718600 | tf_op jit(solution)/shard_map/cond/branch_1_fun/ppermute | solution.py:24
  165.0 32.2 %collective-permute-start.5 = (f32[3,2,2,32768]{3,2,1,0:T(2,128)S(1)}, f32[3,2,2,32768]{3,2,1,0:T(2,128)S(1)}, u32[]{:S(2)}, u32[]{:S(2)}) collective-permute-start(f32[3,2,2,32768]{3,2,1,0:T(2,128)S(1)} %get-tuple-element.67), channel_id=1, source_target_pairs={{0,32},{1,33},{2,34},{3,35},{4,36},{5,37},{6,38},{7,39},{8,40},{9,... | collective-permute-start | bytes 4718600 | tf_op jit(solution)/shard_map/cond/branch_1_fun/ppermute | solution.py:24
  199.6 2.6 %copy-start = (f32[2,1,65536]{2,1,0:T(1,128)S(1)}, f32[2,1,65536]{2,1,0:T(1,128)}, u32[]{:S(2)}) copy-start(f32[2,1,65536]{2,1,0:T(1,128)} %param.23) | copy-start | bytes 1572868
where the time goes:
time: 250 us
  waiting for transfers between devices  161 us (64%)
  blocking collectives  41.3 us (17%)
  other arithmetic  17.6 us (7%)
  local copies, waits for them, and re-layouts  12.3 us (5%)
  starting transfers between devices  11.6 us (5%)
  between operations  5.99 us (2%)
    ppermute x5, waiting for transfers between devices, from_partner(): lax.ppermute(array, axis, [(i, i ^ 1 << apart) for i in range(lax.axis_si...  161 us
    psum x4, blocking collectives, one_axis_at_a_time(): array = lax.psum(array, axis)  41.3 us
    ppermute x5, starting transfers between devices, from_partner(): lax.ppermute(array, axis, [(i, i ^ 1 << apart) for i in range(lax.axis_si...  11.6 us
    rev x1, local copies, waits for them, and re-layouts, shards(): swapped = content[:, :, ::-1, :]  9.74 us
  transfers between devices with their start and end apart: 5, of which 5 were waited for; matrix products, arithmetic and copies ran while one was open for 0% of the time, Pallas kernels for 0%

commit v1 on v0

--- a/solution.py
+++ b/solution.py
@@ -4,6 +4,7 @@
 from jax import lax
 from jax.sharding import Mesh
 from jax.sharding import PartitionSpec as P
+from jax.lax import all_gather
 
 STEP = 100
 ROW_COL = ("row_0", "row_1", "col_0", "col_1")
@@ -16,7 +17,7 @@
 
 def one_axis_at_a_time(array, axes):
     for axis in axes:
-        array = lax.psum(array, axis)
+        array = jnp.sum(all_gather(array, axis), axis=0)
     return array
 
 

time: 250 us -> 258 us (1.032)
  local copies, waits for them, and re-layouts: 12.3 us -> 20.3 us
    psum x4 -> x0, blocking collectives: 41.3 us -> none  [one_axis_at_a_time(): array = lax.psum(array, axis)]
    unnamed x0 -> x4, blocking collectives: none -> 38.8 us
    unnamed x6 -> x26, local copies, waits for them, and re-layouts: 0.02 us -> 7.99 us
where the time goes in v1:
time: 258 us
  waiting for transfers between devices  161 us (62%)
  blocking collectives  38.8 us (15%)
  local copies, waits for them, and re-layouts  20.3 us (8%)
  other arithmetic  20 us (8%)
  starting transfers between devices  11.6 us (4%)
  between operations  6.04 us (2%)
    ppermute x5, waiting for transfers between devices, from_partner(): lax.ppermute(array, axis, [(i, i ^ 1 << apart) for i in range(lax.axis_si...  161 us
    unnamed x4, blocking collectives  38.8 us
    ppermute x5, starting transfers between devices, from_partner(): lax.ppermute(array, axis, [(i, i ^ 1 << apart) for i in range(lax.axis_si...  11.6 us
    rev x1, local copies, waits for them, and re-layouts, shards(): swapped = content[:, :, ::-1, :]  9.74 us
    unnamed x26, local copies, waits for them, and re-layouts  7.99 us
  transfers between devices with their start and end apart: 5, of which 5 were waited for; matrix products, arithmetic and copies ran while one was open for 0% of the time, Pallas kernels for 0%

profile of v1, /device:TPU:1, one launch (start us, length us, event | category | flops | bytes accessed | tf_op | source)
XLA Modules:
  0.0 258.1 jit_solution(4898382784335298163)
XLA Ops:
  0.6 2.0 pad_maximum_fusion
  2.7 9.7 %rev.3 = f32[3,2,2,32768]{3,2,1,0:T(2,128)S(1)} reverse(f32[3,2,2,32768]{3,2,1,0:T(2,128)S(1)} %pad_maximum_fusion), dimensions={2} | reverse | bytes 3145728 | tf_op jit(solution)/shard_map/rev | solution.py:67
  13.1 2.2 broadcast_select_fusion.7
  17.4 36.9 %conditional.8 = (f32[3,2,2,32768]{3,2,1,0:T(2,128)S(1)}) conditional(s32[]{:T(128)} %convert_element_type.26, f32[3,2,2,32768]{3,2,1,0:T(2,128)S(1)} %get-tuple-element.112, (pred[2,1]{1,0:T(4,128)(4,1)S(1)}, f32[3,2,2,32768]{3,2,1,0:T(2,128)S(1)}) %tuple.51), branch_computations={%region_9.10_spmd, %region_10.11_spmd} | conditional | flops 393216 | bytes 11010103 | solution.py:59
  17.4 2.2 collective-permute-start.1
  19.7 33.6 %collective-permute-done.1 = f32[3,2,2,32768]{3,2,1,0:T(2,128)S(1)} collective-permute-done((f32[3,2,2,32768]{3,2,1,0:T(2,128)S(1)}, f32[3,2,2,32768]{3,2,1,0:T(2,128)S(1)}, u32[]{:S(2)}, u32[]{:S(2)}) %collective-permute-start.1) | collective-permute-done | bytes 1572896 | tf_op jit(solution)/shard_map/cond/branch_1_fun/ppermute | solution.py:25
  55.0 37.3 %conditional.9 = (f32[3,2,2,32768]{3,2,1,0:T(2,128)S(1)}) conditional(s32[]{:T(128)} %convert_element_type.25, f32[3,2,2,32768]{3,2,1,0:T(2,128)S(1)} %get-tuple-element.113, (pred[2,1]{1,0:T(4,128)(4,1)S(1)}, f32[3,2,2,32768]{3,2,1,0:T(2,128)S(1)}) %tuple.52), branch_computations={%region_11.12_spmd, %region_12.13_spmd} | conditional | flops 393216 | bytes 11010103 | solution.py:59
  55.0 3.2 %collective-permute-start.2 = (f32[3,2,2,32768]{3,2,1,0:T(2,128)S(1)}, f32[3,2,2,32768]{3,2,1,0:T(2,128)S(1)}, u32[]{:S(2)}, u32[]{:S(2)}) collective-permute-start(f32[3,2,2,32768]{3,2,1,0:T(2,128)S(1)} %get-tuple-element.61), channel_id=1, source_target_pairs={{0,4},{1,5},{2,6},{3,7},{4,0},{5,1},{6,2},{7,3},{8,12},{9,13},{10,... | collective-permute-start | bytes 4718600 | tf_op jit(solution)/shard_map/cond/branch_1_fun/ppermute | solution.py:25
  58.4 33.0 %collective-permute-done.2 = f32[3,2,2,32768]{3,2,1,0:T(2,128)S(1)} collective-permute-done((f32[3,2,2,32768]{3,2,1,0:T(2,128)S(1)}, f32[3,2,2,32768]{3,2,1,0:T(2,128)S(1)}, u32[]{:S(2)}, u32[]{:S(2)}) %collective-permute-start.2) | collective-permute-done | bytes 1572896 | tf_op jit(solution)/shard_map/cond/branch_1_fun/ppermute | solution.py:25
  92.9 35.0 %conditional.10 = (f32[3,2,2,32768]{3,2,1,0:T(2,128)S(1)}) conditional(s32[]{:T(128)} %convert_element_type.24, f32[3,2,2,32768]{3,2,1,0:T(2,128)S(1)} %get-tuple-element.114, (pred[2,1]{1,0:T(4,128)(4,1)S(1)}, f32[3,2,2,32768]{3,2,1,0:T(2,128)S(1)}) %tuple.53), branch_computations={%region_13.14_spmd, %region_14.15_spmd} | conditional | flops 393216 | bytes 11010103 | solution.py:59
  93.0 1.7 collective-permute-start.3
  94.7 32.2 %collective-permute-done.3 = f32[3,2,2,32768]{3,2,1,0:T(2,128)S(1)} collective-permute-done((f32[3,2,2,32768]{3,2,1,0:T(2,128)S(1)}, f32[3,2,2,32768]{3,2,1,0:T(2,128)S(1)}, u32[]{:S(2)}, u32[]{:S(2)}) %collective-permute-start.3) | collective-permute-done | bytes 1572896 | tf_op jit(solution)/shard_map/cond/branch_1_fun/ppermute | solution.py:25
  128.6 35.8 %conditional.11 = (f32[3,2,2,32768]{3,2,1,0:T(2,128)S(1)}) conditional(s32[]{:T(128)} %convert_element_type.23, f32[3,2,2,32768]{3,2,1,0:T(2,128)S(1)} %get-tuple-element.115, (pred[2,1]{1,0:T(4,128)(4,1)S(1)}, f32[3,2,2,32768]{3,2,1,0:T(2,128)S(1)}) %tuple.54), branch_computations={%region_15.16_spmd, %region_16.17_spmd} | conditional | flops 393216 | bytes 11010103 | solution.py:59
  128.6 3.3 %collective-permute-start.4 = (f32[3,2,2,32768]{3,2,1,0:T(2,128)S(1)}, f32[3,2,2,32768]{3,2,1,0:T(2,128)S(1)}, u32[]{:S(2)}, u32[]{:S(2)}) collective-permute-start(f32[3,2,2,32768]{3,2,1,0:T(2,128)S(1)} %get-tuple-element.65), channel_id=1, source_target_pairs={{0,16},{1,17},{2,18},{3,19},{4,20},{5,21},{6,22},{7,23},{8,24},{9,... | collective-permute-start | bytes 4718600 | tf_op jit(solution)/shard_map/cond/branch_1_fun/ppermute | solution.py:25
  132.0 31.4 %collective-permute-done.4 = f32[3,2,2,32768]{3,2,1,0:T(2,128)S(1)} collective-permute-done((f32[3,2,2,32768]{3,2,1,0:T(2,128)S(1)}, f32[3,2,2,32768]{3,2,1,0:T(2,128)S(1)}, u32[]{:S(2)}, u32[]{:S(2)}) %collective-permute-start.4) | collective-permute-done | bytes 1572896 | tf_op jit(solution)/shard_map/cond/branch_1_fun/ppermute | solution.py:25
  165.0 33.2 %conditional.12 = (f32[3,2,2,32768]{3,2,1,0:T(2,128)S(1)}) conditional(s32[]{:T(128)} %convert_element_type.22, f32[3,2,2,32768]{3,2,1,0:T(2,128)S(1)} %get-tuple-element.116, (pred[2,1]{1,0:T(4,128)(4,1)S(1)}, f32[3,2,2,32768]{3,2,1,0:T(2,128)S(1)}) %tuple.55), branch_computations={%region_17.18_spmd, %region_18.19_spmd} | conditional | flops 393216 | bytes 11010103 | solution.py:59
  166.4 30.8 %collective-permute-done.5 = f32[3,2,2,32768]{3,2,1,0:T(2,128)S(1)} collective-permute-done((f32[3,2,2,32768]{3,2,1,0:T(2,128)S(1)}, f32[3,2,2,32768]{3,2,1,0:T(2,128)S(1)}, u32[]{:S(2)}, u32[]{:S(2)}) %collective-permute-start.5) | collective-permute-done | bytes 1572896 | tf_op jit(solution)/shard_map/cond/branch_1_fun/ppermute | solution.py:25
  202.8 1.7 multiply_reduce_fusion
  204.5 1.4 dynamic-update-slice
  205.9 8.4 %all-reduce = f32[4]{0:T(128)S(1)} all-reduce(f32[4]{0:T(128)S(1)} %dynamic-update-slice), channel_id=1, replica_groups=mesh['row_0'=4,'row_1'=4,'col_0'=4,'col_1'=2] {'row_0'}, use_global_device_ids=true, to_apply=%add | all-reduce | flops 4 | bytes 32
  217.0 8.5 %all-reduce.1 = f32[4]{0:T(128)S(1)} all-reduce(f32[4]{0:T(128)S(1)} %dynamic-update-slice.1), channel_id=1, replica_groups=mesh['row_0'=4,'row_1'=4,'col_0'=4,'col_1'=2] {'row_1'}, use_global_device_ids=true, to_apply=%add.1 | all-reduce | flops 4 | bytes 32
  228.1 8.7 %all-reduce.2 = f32[4]{0:T(128)S(1)} all-reduce(f32[4]{0:T(128)S(1)} %dynamic-update-slice.2), channel_id=1, replica_groups=mesh['row_0'=4,'row_1'=4,'col_0'=4,'col_1'=2] {'col_0'}, use_global_device_ids=true, to_apply=%add.2 | all-reduce | flops 4 | bytes 32
  239.4 13.1 %all-reduce.3 = f32[2]{0:T(128)S(1)} all-reduce(f32[2]{0:T(128)S(1)} %dynamic-update-slice.3), channel_id=1, replica_groups=mesh['row_0'=4,'row_1'=4,'col_0'=4,'col_1'=2] {'col_1'}, use_global_device_ids=true, to_apply=%add.3 | all-reduce | flops 2 | bytes 16
  253.8 4.3 %multiply_subtract_fusion = (f32[2,1,65536]{2,1,0:T(1,128)}, f32[2,1,65536]{2,1,0:T(1,128)}, f32[2,1,65536]{2,1,0:T(1,128)}) fusion(f32[2,1,65536]{2,1,0:T(1,128)S(1)} %squeeze.2, f32[2,1,65536]{2,1,0:T(1,128)S(1)} %mul.74, f32[2,1,65536]{2,1,0:T(1,128)S(1)} %copy-done, f32[]{:T(128)S(6)} %div.18, f32[2,1,65536]{2,1,0:T(1,128)S(1)} %mul.81), kind=kLoop, calls=%fused_computation.13 | loop fusion | flops 1835008 | bytes 3670020 | tf_op jit(solution)/shard_map/sub | solution.py:35
  (48 shorter events, 20.5 us)
Async XLA Ops:
  2.7 9.8 %copy-start.1 = (s32[2,128]{1,0:T(2,128)S(1)}, s32[2,128]{1,0:T(2,128)}, u32[]{:S(2)}) copy-start(s32[2,128]{1,0:T(2,128)} %param.25) | copy-start | bytes 3076
  2.7 9.8 %copy-start.2 = (s32[2,256]{1,0:T(2,128)S(1)}, s32[2,256]{1,0:T(2,128)}, u32[]{:S(2)}) copy-start(s32[2,256]{1,0:T(2,128)} %param.24) | copy-start | bytes 6148
  17.4 36.0 %collective-permute-start.1 = (f32[3,2,2,32768]{3,2,1,0:T(2,128)S(1)}, f32[3,2,2,32768]{3,2,1,0:T(2,128)S(1)}, u32[]{:S(2)}, u32[]{:S(2)}) collective-permute-start(f32[3,2,2,32768]{3,2,1,0:T(2,128)S(1)} %get-tuple-element.59), channel_id=1, source_target_pairs={{0,2},{1,3},{2,0},{3,1},{4,6},{5,7},{6,4},{7,5},{8,10},{9,11},{10,... | collective-permute-start | bytes 4718600 | tf_op jit(solution)/shard_map/cond/branch_1_fun/ppermute | solution.py:25
  55.0 36.3 %collective-permute-start.2 = (f32[3,2,2,32768]{3,2,1,0:T(2,128)S(1)}, f32[3,2,2,32768]{3,2,1,0:T(2,128)S(1)}, u32[]{:S(2)}, u32[]{:S(2)}) collective-permute-start(f32[3,2,2,32768]{3,2,1,0:T(2,128)S(1)} %get-tuple-element.61), channel_id=1, source_target_pairs={{0,4},{1,5},{2,6},{3,7},{4,0},{5,1},{6,2},{7,3},{8,12},{9,13},{10,... | collective-permute-start | bytes 4718600 | tf_op jit(solution)/shard_map/cond/branch_1_fun/ppermute | solution.py:25
  93.0 34.0 %collective-permute-start.3 = (f32[3,2,2,32768]{3,2,1,0:T(2,128)S(1)}, f32[3,2,2,32768]{3,2,1,0:T(2,128)S(1)}, u32[]{:S(2)}, u32[]{:S(2)}) collective-permute-start(f32[3,2,2,32768]{3,2,1,0:T(2,128)S(1)} %get-tuple-element.63), channel_id=1, source_target_pairs={{0,8},{1,9},{2,10},{3,11},{4,12},{5,13},{6,14},{7,15},{8,0},{9,1},... | collective-permute-start | bytes 4718600 | tf_op jit(solution)/shard_map/cond/branch_1_fun/ppermute | solution.py:25
  128.6 34.8 %collective-permute-start.4 = (f32[3,2,2,32768]{3,2,1,0:T(2,128)S(1)}, f32[3,2,2,32768]{3,2,1,0:T(2,128)S(1)}, u32[]{:S(2)}, u32[]{:S(2)}) collective-permute-start(f32[3,2,2,32768]{3,2,1,0:T(2,128)S(1)} %get-tuple-element.65), channel_id=1, source_target_pairs={{0,16},{1,17},{2,18},{3,19},{4,20},{5,21},{6,22},{7,23},{8,24},{9,... | collective-permute-start | bytes 4718600 | tf_op jit(solution)/shard_map/cond/branch_1_fun/ppermute | solution.py:25
  165.0 32.2 %collective-permute-start.5 = (f32[3,2,2,32768]{3,2,1,0:T(2,128)S(1)}, f32[3,2,2,32768]{3,2,1,0:T(2,128)S(1)}, u32[]{:S(2)}, u32[]{:S(2)}) collective-permute-start(f32[3,2,2,32768]{3,2,1,0:T(2,128)S(1)} %get-tuple-element.67), channel_id=1, source_target_pairs={{0,32},{1,33},{2,34},{3,35},{4,36},{5,37},{6,38},{7,39},{8,40},{9,... | collective-permute-start | bytes 4718600 | tf_op jit(solution)/shard_map/cond/branch_1_fun/ppermute | solution.py:25
  199.6 2.7 %copy-start.6 = (u32[128]{0:T(128)S(1)}, u32[128]{0:T(128)}, u32[]{:S(2)}) copy-start(u32[128]{0:T(128)} %constant.44) | copy-start | bytes 1540
  199.6 3.2 %copy-start = (f32[2,1,65536]{2,1,0:T(1,128)S(1)}, f32[2,1,65536]{2,1,0:T(1,128)}, u32[]{:S(2)}) copy-start(f32[2,1,65536]{2,1,0:T(1,128)} %param.23) | copy-start | bytes 1572868
  200.5 14.5 %copy-start.5 = (u32[128]{0:T(128)S(1)}, u32[128]{0:T(128)}, u32[]{:S(2)}) copy-start(u32[128]{0:T(128)} %constant.49) | copy-start | bytes 1540
  200.5 25.6 %copy-start.4 = (u32[128]{0:T(128)S(1)}, u32[128]{0:T(128)}, u32[]{:S(2)}) copy-start(u32[128]{0:T(128)} %constant.54) | copy-start | bytes 1540
  200.5 36.9 %copy-start.3 = (u32[128]{0:T(128)S(1)}, u32[128]{0:T(128)}, u32[]{:S(2)}) copy-start(u32[128]{0:T(128)} %constant.59) | copy-start | bytes 1540
